TPU v7x, 16 devices: a 4x2x1 block of a 4x4x4 slice. The times are simulated.
16 devices in a mesh: dp: 2 (over y, z), tp: 8 (over x, core).
Axes of the slice: x: 4, y: 2, z: 1, core: 2. Of those that a mesh axis runs over, the one named last changes fastest.
The devices are a block of a 4x4x4 slice.
Arguments:
- x: bfloat16 [128, 2048], P('dp'), parts along dimension 0
- k_cache: bfloat16 [128, 4096, 32, 64], P('dp', None, 'tp'), parts along dimension 0
- v_cache: bfloat16 [128, 4096, 32, 64], P('dp', None, 'tp'), parts along dimension 0
- gain_a: bfloat16 [2048], replicated
- wq: bfloat16 [2048, 2048], P(None, 'tp')
- wo: bfloat16 [2048, 2048], P('tp')
- gain_m: bfloat16 [2048], replicated
- w_gate: bfloat16 [2048, 5120], P(None, 'tp')
- w_up: bfloat16 [2048, 5120], P(None, 'tp')
- w_down: bfloat16 [5120, 2048], P('tp')
Outputs:
- output: bfloat16 [128, 2048], P('dp'), parts along dimension 0
There are 2 independent parts. A program takes and returns all parts, laid end to end along the dimension named above; an argument that names none is the same for every part.
All inputs are finite; a program needn't handle non-finite values.
Results may differ from a plain program's by a relative error of at most 0.017.
Values are sent between devices in bfloat16 or wider.
A program may use at most 1.5 GiB of HBM per device.

v0:
```python
import functools
import math

import jax
import jax.numpy as jnp
import numpy as np
from jax import lax
from jax.experimental import pallas as pl
from jax.experimental.pallas import tpu as pltpu
from jax.sharding import PartitionSpec as P

HEAD = 64
THETA = 10000
MESH = pl.DeviceIdType.MESH

SLOTS = 4
EARLY = 2
CHUNKS = ((52, (0, 4, 8, 12.1, 16.1)), (8, (0, 4.2, 8.2)), (4, (0, 4, 8)))
ROWS = 8
LANES = 128


def turns(heads, place):
    half = HEAD // 2
    angle = np.float32(place) * np.float32(THETA) ** (-np.arange(half, dtype=np.float32) / np.float32(half))
    angle = angle.astype(np.float64)
    cos, sin = np.cos(angle), np.sin(angle)
    own, other = np.concatenate([cos, cos]), np.concatenate([-sin, sin])
    return np.stack([np.tile(own, heads), np.tile(other, heads)]).astype(np.float32)


def scaled(wide, gain):
    scale = lax.rsqrt(jnp.mean(wide * wide, -1, keepdims=True) + 1e-6)
    return (wide * scale * gain).astype(jnp.bfloat16)


def blocks(rows):
    return [(r, min(ROWS, rows - r)) for r in range(0, rows, ROWS)]


def added(parts):
    while len(parts) > 1:
        parts = [a + b for a, b in zip(parts[::2], parts[1::2])] + parts[len(parts) & ~1:]
    return parts[0]


def kernel(n, chunks, x_hbm, k_hbm, v_hbm, ga_hbm, wq_hbm, wo_hbm, gm_hbm, wg_hbm, wu_hbm, wd_hbm, turn_hbm, y_hbm,
           x, ga, wq, wo, gm, wg, wu, wd, turn, kbuf, vbuf, query, weights, seen, normal, y,
           terms, parts, h, sums, first_sem, later_sem, ksem, vsem, ysem, send_sem, recv_sem):
    batch, d = x.shape
    width = wq.shape[1]
    share = d // n
    me = lax.axis_index("tp")
    mine = pl.ds(pl.multiple_of(me * share, share), share)
    row_of = lax.broadcasted_iota(jnp.int32, (ROWS, width), 0)
    head_of = lax.broadcasted_iota(jnp.int32, (ROWS, width), 1) // HEAD
    own = row_of == head_of

    first = [pltpu.make_async_copy(a, b, first_sem.at[i])
             for i, (a, b) in enumerate(((x_hbm, x), (ga_hbm, ga), (turn_hbm, turn), (wq_hbm, wq)))]
    later = [pltpu.make_async_copy(a, b, later_sem.at[i])
             for i, (a, b) in enumerate(((wo_hbm, wo), (gm_hbm, gm), (wg_hbm, wg), (wu_hbm, wu), (wd_hbm, wd)))]

    def keys(i):
        slot = lax.rem(i, SLOTS)
        return pltpu.make_async_copy(k_hbm.at[i], kbuf.at[slot], ksem.at[slot])

    def values(i):
        slot = lax.rem(i, SLOTS)
        return pltpu.make_async_copy(v_hbm.at[i], vbuf.at[slot], vsem.at[slot])

    def peer(k):
        return lax.rem(me + k, n)

    def remote(step, c, k, source, target):
        return pltpu.make_async_remote_copy(
            src_ref=source, dst_ref=target, send_sem=send_sem.at[step, c, k - 1], recv_sem=recv_sem.at[step, c, k - 1],
            device_id={"tp": peer(k)}, device_id_type=MESH)

    def start(copies):
        for copy in copies:
            copy.start()

    def wait(copies):
        for copy in copies:
            copy.wait_send()
            copy.wait_recv()

    def wide_gain(g):
        g = g[...].astype(jnp.float32)
        return jnp.concatenate([g[i:i + 1] for i in range(g.shape[0])], 1)

    def attend_keys(i):
        slot = lax.rem(i, SLOTS)
        q = jnp.where(own, jnp.broadcast_to(query[pl.ds(i, 1), :], (ROWS, width)), 0.0).astype(jnp.bfloat16)
        scores = jnp.dot(q, kbuf[slot], preferred_element_type=jnp.float32)
        top = jnp.max(scores, -1, keepdims=True)
        p = jnp.exp2((scores - top) * (HEAD**-0.5 * math.log2(math.e)))
        p = p * (1.0 / jnp.sum(p, -1, keepdims=True))
        return p.astype(jnp.bfloat16)

    def attend_values(i, w):
        slot = lax.rem(i, SLOTS)
        o = lax.dot_general(w, vbuf[slot], (((1,), (1,)), ((), ())), preferred_element_type=jnp.float32)
        o = jnp.sum(jnp.where(own, o, 0.0), 0, keepdims=True)
        seen[pl.ds(i, 1), :] = o

    def attended(c):
        at, rows, _ = chunks[c]
        return jnp.dot(seen[pl.ds(at, rows), :].astype(jnp.bfloat16), wo[...], preferred_element_type=jnp.float32).astype(jnp.bfloat16)

    def fed(b):
        gate = jnp.dot(b, wg[...], preferred_element_type=jnp.float32)
        up = jnp.dot(b, wu[...], preferred_element_type=jnp.float32)
        hidden = (jax.nn.silu(gate) * up).astype(jnp.bfloat16)
        return jnp.dot(hidden, wd[...], preferred_element_type=jnp.float32).astype(jnp.bfloat16)

    def y_copy(c):
        at, rows, _ = chunks[c]
        on = pl.ds(at // ROWS * ROWS, (at + rows) // ROWS * ROWS - at // ROWS * ROWS)
        return None

    def scatter(half, c):
        return [remote(2 * half, c, k, terms[c].at[half, :, pl.ds(pl.multiple_of(peer(k) * share, share), share)],
                       parts[c].at[half, k - 1]) for k in range(1, n)]

    def gather(half, c):
        block = (h, sums)[half][c].at[:, mine]
        return [remote(2 * half + 1, c, k, block, block) for k in range(1, n)]

    def scattered(half, c, value):
        terms[c][half] = value
        start(scatter(half, c))

    def reduced(half, c):
        wait(scatter(half, c))
        at, rows, _ = chunks[c]
        for r, m in blocks(rows):
            on = pl.ds(r, m)
            total = added([terms[c][half, on, mine].astype(jnp.float32)]
                          + [parts[c][half, k, on, :].astype(jnp.float32) for k in range(n - 1)])
            t = h[c][on, mine] if half else x[pl.ds(at + r, m), mine]
            (h, sums)[half][c][on, mine] = (t.astype(jnp.float32) + total).astype(jnp.bfloat16)
        start(gather(half, c))

    def project(c):
        scattered(0, c, attended(c))

    def feed(c):
        wait(gather(0, c))
        at, rows, _ = chunks[c]
        gain = wide_gain(gm)
        for r, m in blocks(rows):
            normal[pl.ds(r, m), :] = scaled(h[c][pl.ds(r, m), :].astype(jnp.float32), gain)
        scattered(1, c, fed(normal[pl.ds(0, rows), :]))

    def finish(c):
        wait(gather(1, c))
        at, rows, _ = chunks[c]
        y_hbm[pl.ds(at, rows), :] = sums[c][...]
        pass

    def shout(half, c):
        return [remote(2 * half, c, k, terms[c].at[half], parts[c].at[half, me]) for k in range(1, n)]

    def shouted(half, c, value):
        terms[c][half] = value
        parts[c][half, me] = value
        start(shout(half, c))

    def heard(half, c, t):
        wait(shout(half, c))
        total = added([parts[c][half, s].astype(jnp.float32) for s in range(n)])
        return (t.astype(jnp.float32) + total).astype(jnp.bfloat16)

    def small_project(c):
        shouted(0, c, attended(c))

    def small_feed(c):
        at, rows, _ = chunks[c]
        now = heard(0, c, x[pl.ds(at, rows), :])
        h[c][...] = now
        shouted(1, c, fed(scaled(now.astype(jnp.float32), wide_gain(gm))))

    def small_finish(c):
        at, rows, _ = chunks[c]
        y_hbm[pl.ds(at, rows), :] = heard(1, c, h[c][...])
        pass

    start(first)
    keys(0).start()
    for i in range(1, EARLY):
        keys(i).start()
        values(i - 1).start()
    barrier = pltpu.get_barrier_semaphore()
    for k in range(1, n):
        pl.semaphore_signal(barrier, inc=1, device_id={"tp": peer(k)}, device_id_type=MESH)

    for copy in first:
        copy.wait()
    for i in range(EARLY, SLOTS):
        keys(i).start()
        values(i - 1).start()
    values(SLOTS - 1).start()
    gain = wide_gain(ga)
    for r, m in blocks(batch):
        normal[pl.ds(r, m), :] = scaled(x[pl.ds(r, m), :].astype(jnp.float32), gain)
    q = jnp.dot(normal[...], wq[...], preferred_element_type=jnp.float32).astype(jnp.bfloat16).astype(jnp.float32)
    lane = lax.broadcasted_iota(jnp.int32, q.shape, 1)
    other = jnp.where(lane % HEAD < HEAD // 2, pltpu.roll(q, width - HEAD // 2, 1), pltpu.roll(q, HEAD // 2, 1))
    query[...] = (q * turn[0:1, :] + other * turn[1:2, :]).astype(jnp.bfloat16).astype(jnp.float32)

    pl.semaphore_wait(barrier, n - 1)

    steps = []
    for c, (at, rows, offsets) in enumerate(chunks):
        each = (small_project, small_feed, small_finish)
        if len(offsets) > len(each):
            each = (project, functools.partial(reduced, 0), feed, functools.partial(reduced, 1), finish)
        steps += [(at + rows + offset, functools.partial(f, c)) for offset, f in zip(offsets, each)]
    steps.sort(key=lambda step: step[0])
    events = {}
    for at, f in steps:
        if math.ceil(at) < batch:
            events.setdefault(math.ceil(at), []).append(f)

    keys(0).wait()
    weights[...] = attend_keys(0)
    keys(SLOTS).start()

    @pl.loop(1, batch)
    def _(i):
        keys(i).wait()
        values(i - 1).wait()
        attend_values(i - 1, weights[...])
        weights[...] = attend_keys(i)

        @pl.when(i + SLOTS < batch)
        def _():
            keys(i + SLOTS).start()

        @pl.when(i - 1 + SLOTS < batch)
        def _():
            values(i - 1 + SLOTS).start()

        @pl.when(i == 8)
        def _():
            start(later)

        @pl.when(i == 16)
        def _():
            for copy in later:
                copy.wait()

        for at, what in events.items():
            @pl.when(i == at)
            def _():
                for f in what:
                    f()

    values(batch - 1).wait()
    attend_values(batch - 1, weights[...])
    for at, f in steps:
        if math.ceil(at) >= batch:
            f()
    for c in range(len(chunks)):
        pass


def solution(mesh):
    n = mesh.shape["tp"]

    def step(x, k_cache, v_cache, gain_a, wq, wo, gain_m, w_gate, w_up, w_down):
        batch, cache, heads, head = k_cache.shape
        d, width, hidden = x.shape[1], wq.shape[1], w_gate.shape[1]
        chunks, at = [], 0
        for rows, offsets in CHUNKS:
            chunks.append((at, rows, offsets))
            at += rows
        assert at == batch
        flat = lambda t: jnp.transpose(t, (0, 2, 3, 1)).reshape(batch, heads * head, cache)
        bf16, f32 = jnp.bfloat16, jnp.float32
        operands = (x, flat(k_cache), flat(v_cache), gain_a.reshape(-1, LANES), wq, wo, gain_m.reshape(-1, LANES), w_gate, w_up, w_down,
                    jnp.asarray(turns(heads, cache - 1)))
        scratch = [
            pltpu.VMEM((batch, d), bf16), pltpu.VMEM((d // LANES, LANES), bf16), pltpu.VMEM(wq.shape, bf16), pltpu.VMEM(wo.shape, bf16),
            pltpu.VMEM((d // LANES, LANES), bf16), pltpu.VMEM(w_gate.shape, bf16), pltpu.VMEM(w_up.shape, bf16), pltpu.VMEM(w_down.shape, bf16),
            pltpu.VMEM((2, width), f32),
            pltpu.VMEM((SLOTS, width, cache), bf16), pltpu.VMEM((SLOTS, width, cache), bf16),
            pltpu.VMEM((batch, width), f32), pltpu.VMEM((ROWS, cache), bf16), pltpu.VMEM((batch, width), f32),
            pltpu.VMEM((batch, d), bf16), pltpu.VMEM((batch, d), bf16),
            [pltpu.VMEM((2, r, d), bf16) for _, r, _ in chunks],
            [pltpu.VMEM((2, n, r, d), bf16) if len(o) < 5 else pltpu.VMEM((2, n - 1, r, d // n), bf16) for _, r, o in chunks],
            [pltpu.VMEM((r, d), bf16) for _, r, _ in chunks], [pltpu.VMEM((r, d), bf16) for _, r, _ in chunks],
            pltpu.SemaphoreType.DMA((4,)), pltpu.SemaphoreType.DMA((5,)),
            pltpu.SemaphoreType.DMA((SLOTS,)), pltpu.SemaphoreType.DMA((SLOTS,)), pltpu.SemaphoreType.DMA((len(chunks),)),
            pltpu.SemaphoreType.DMA((4, len(chunks), n - 1)), pltpu.SemaphoreType.DMA((4, len(chunks), n - 1)),
        ]
        return pl.pallas_call(
            functools.partial(kernel, n, chunks),
            out_shape=pltpu.VMEM((batch, d), bf16),
            in_specs=[pl.BlockSpec(memory_space=pl.ANY)] * len(operands),
            out_specs=pl.BlockSpec(memory_space=pltpu.VMEM),
            scratch_shapes=scratch,
            compiler_params=pltpu.CompilerParams(collective_id=0, has_side_effects=True, vmem_limit_bytes=56 * 2**20),
            cost_estimate=pl.CostEstimate(flops=2 * batch * width * cache * 4, bytes_accessed=4 * batch * width * cache, transcendentals=0),
            name="layer",
        )(*operands)

    states, cache, columns, rows_of = P("dp", None), P("dp", None, "tp", None), P(None, "tp"), P("tp", None)
    return jax.shard_map(
        step,
        mesh=mesh,
        in_specs=(states, cache, cache, P(None), columns, rows_of, P(None), columns, columns, rows_of),
        out_specs=states,
        check_vma=False,
    )
```

profile of v0, /device:TPU:113, one launch (start us, length us, event | category | flops | bytes accessed | tf_op | source)
XLA Modules:
  0.0 101.6 jit_solution(10237160781994155710)
XLA Ops:
  0.0 100.9 %layer.1 = bf16[64,2048]{1,0:T(8,128)(2,1)S(1)} custom-call(bf16[64,2048]{1,0:T(8,128)(2,1)} %x_hbm.1, bf16[64,256,4096]{2,1,0:T(8,128)(2,1)} %bitcast.1.k_hbm, bf16[64,256,4096]{2,1,0:T(8,128)(2,1)} %bitcast.3.v_hbm, bf16[16,128]{1,0:T(8,128)(2,1)} %bitcast.8, bf16[2048,256]{1,0:T(8,128)(2,1)} %wq_hbm.1, bf16[256,2048]{1,0:T(8,128)(2,1)} %wo_hbm.1, ...), custom_call_target="tpu_custom_call" | custom-call | flops 536870912 | bytes 268435456 | tf_op jit(solution)/shard_map/layer/pallas_call | solution.py:299
  100.9 0.7 copy.13
where the time goes:
time: 102 us
  Pallas kernels  101 us (99%)
    pallas_call x1, Pallas kernels, step(): pl.pallas_call(functools.partial(kernel, n, chunks), out_shape=pltpu.VMEM...  101 us

commit v1 on v0

--- a/solution.py
+++ b/solution.py
@@ -50,6 +50,7 @@
     batch, d = x.shape
     width = wq.shape[1]
     share = d // n
+    others = sorted(range(1, n), key=lambda k: abs(n - 2 * k))
     me = lax.axis_index("tp")
     mine = pl.ds(pl.multiple_of(me * share, share), share)
     row_of = lax.broadcasted_iota(jnp.int32, (ROWS, width), 0)
@@ -122,11 +123,11 @@
 
     def scatter(half, c):
         return [remote(2 * half, c, k, terms[c].at[half, :, pl.ds(pl.multiple_of(peer(k) * share, share), share)],
-                       parts[c].at[half, k - 1]) for k in range(1, n)]
+                       parts[c].at[half, k - 1]) for k in others]
 
     def gather(half, c):
         block = (h, sums)[half][c].at[:, mine]
-        return [remote(2 * half + 1, c, k, block, block) for k in range(1, n)]
+        return [remote(2 * half + 1, c, k, block, block) for k in others]
 
     def scattered(half, c, value):
         terms[c][half] = value
@@ -161,7 +162,7 @@
         pass
 
     def shout(half, c):
-        return [remote(2 * half, c, k, terms[c].at[half], parts[c].at[half, me]) for k in range(1, n)]
+        return [remote(2 * half, c, k, terms[c].at[half], parts[c].at[half, me]) for k in others]
 
     def shouted(half, c, value):
         terms[c][half] = value
@@ -232,8 +233,10 @@
     def _(i):
         keys(i).wait()
         values(i - 1).wait()
-        attend_values(i - 1, weights[...])
-        weights[...] = attend_keys(i)
+        old = weights[...]
+        new = attend_keys(i)
+        attend_values(i - 1, old)
+        weights[...] = new
 
         @pl.when(i + SLOTS < batch)
         def _():

time: 102 us -> 101 us (level)
  no operation moved by 1% of the time
where the time goes in v1:
time: 101 us
  Pallas kernels  100 us (99%)
    pallas_call x1, Pallas kernels, step(): pl.pallas_call(functools.partial(kernel, n, chunks), out_shape=pltpu.VMEM...  100 us

profile of v1, /device:TPU:113, one launch (start us, length us, event | category | flops | bytes accessed | tf_op | source)
XLA Modules:
  0.0 100.9 jit_solution(1321546254499919700)
XLA Ops:
  0.0 100.2 %layer.1 = bf16[64,2048]{1,0:T(8,128)(2,1)S(1)} custom-call(bf16[64,2048]{1,0:T(8,128)(2,1)} %x_hbm.1, bf16[64,256,4096]{2,1,0:T(8,128)(2,1)} %bitcast.1.k_hbm, bf16[64,256,4096]{2,1,0:T(8,128)(2,1)} %bitcast.3.v_hbm, bf16[16,128]{1,0:T(8,128)(2,1)} %bitcast.8, bf16[2048,256]{1,0:T(8,128)(2,1)} %wq_hbm.1, bf16[256,2048]{1,0:T(8,128)(2,1)} %wo_hbm.1, ...), custom_call_target="tpu_custom_call" | custom-call | flops 536870912 | bytes 268435456 | tf_op jit(solution)/shard_map/layer/pallas_call | solution.py:302
  100.2 0.7 copy.13
